TPU v7x, 32 devices: a whole 2x2x4 slice. The times are simulated.
32 devices in a mesh: gx: 8 (over z, x), col: 4 (over y, core).
Axes of the slice: x: 2, y: 2, z: 4, core: 2. Of those that a mesh axis runs over, the one named last changes fastest.
Arguments:
- grid_field: bfloat16 [64, 32, 256, 128], P('col', 'gx'), may hold values from -6 to 6
- tucker_core: float32 [2, 32, 32, 8, 8, 4], P(None, 'col'), may hold values from -0.5 to 0.5
- in_factor: float32 [64, 32], P('col'), may hold values from -0.75 to 0.75
- out_factor: float32 [64, 32], P('col'), may hold values from -1 to 1
- x_factor: float32 [32, 8], replicated, may hold values from -4 to 4
- y_factor: float32 [32, 8], replicated, may hold values from -4 to 4
- z_factor: float32 [16, 4], replicated, may hold values from -4 to 4
- kx_reach: int32 [32, 16], replicated, may hold values from 1 to 17
Outputs:
- spectral_out: bfloat16 [64, 32, 256, 128], P('col', 'gx')
All inputs are finite; a program needn't handle non-finite values.
Results may differ from a plain program's by a relative error of at most 0.001.
Values sent between devices are 32-bit elements; how exact they have to be, the bound alone decides.
A program may use at most 64 MiB of HBM per device.

v0:
```python
import math
import jax
import jax.numpy as jnp
from jax import lax
from jax.sharding import PartitionSpec as P


def slot_freq(slot_count):
    slot_index = jnp.arange(slot_count, dtype=jnp.int32)
    return jnp.where(slot_index < slot_count // 2, slot_index, slot_index - slot_count)


def phase_table(positions, extent, slot_count, direction):
    phase_steps = positions[:, None] * slot_freq(slot_count)[None, :] % extent
    radians = 2.0 * math.pi / extent * phase_steps.astype(jnp.float32)
    norm_scale = 1.0 / math.sqrt(extent)
    cosine = jnp.cos(radians) * norm_scale
    sine_part = direction * jnp.sin(radians) * norm_scale
    return jnp.stack([jnp.stack([cosine, -sine_part], 1), jnp.stack([sine_part, cosine], 1)], 1)


def z_tables(grid_z, modes_z):
    z_index = jnp.arange(grid_z, dtype=jnp.int32)
    kz_index = jnp.arange(modes_z, dtype=jnp.int32)
    phase_steps = z_index[:, None] * kz_index[None, :] % grid_z
    radians = 2.0 * math.pi / grid_z * phase_steps.astype(jnp.float32)
    norm_scale = 1.0 / math.sqrt(grid_z)
    cosine = jnp.cos(radians) * norm_scale
    sine_part = jnp.sin(radians) * norm_scale
    forward = jnp.stack([cosine, -sine_part], 1)
    weight = jnp.where(kz_index == 0, 1.0, 2.0).astype(jnp.float32)
    backward = jnp.stack([(cosine * weight[None, :]).T, -(sine_part * weight[None, :]).T], 0)
    return (forward, backward)


def per_device(
    grid_field, tucker_core, in_factor, out_factor, x_factor, y_factor, z_factor, kx_reach
):
    highest = lax.Precision.HIGHEST
    channels, planes, grid_y, grid_z = grid_field.shape
    modes_x = x_factor.shape[0]
    modes_y = y_factor.shape[0]
    modes_z = z_factor.shape[0]
    width_gx = lax.axis_size("gx")
    grid_x = planes * width_gx
    columns = modes_y * modes_z
    col_dev = columns // width_gx
    slab_index = lax.axis_index("gx")
    z_forward, z_backward = z_tables(grid_z, modes_z)
    y_forward = phase_table(jnp.arange(grid_y, dtype=jnp.int32), grid_y, modes_y, 1.0)
    x_forward = phase_table(jnp.arange(grid_x, dtype=jnp.int32), grid_x, modes_x, 1.0)
    values = grid_field.astype(jnp.float32)
    z_spectrum = jnp.einsum("cxyz,zpl->cxply", values, z_forward, precision=highest)
    y_spectrum = jnp.einsum("cxply,ypqj->qcxjl", z_spectrum, y_forward, precision=highest)
    y_spectrum = y_spectrum.reshape(2, channels, planes, columns)
    first_col = slab_index * col_dev
    reach_dev = lax.dynamic_slice_in_dim(kx_reach.reshape(-1), first_col, col_dev)
    kept_mask = (jnp.abs(slot_freq(modes_x))[:, None] < reach_dev[None, :]).astype(jnp.float32)
    arrived = lax.all_to_all(y_spectrum, "gx", split_axis=3, concat_axis=2, tiled=True)
    spectrum = jnp.einsum("pcxm,xpqk->qckm", arrived, x_forward, precision=highest)
    partial_value = jnp.einsum("qckm,cr->qrkm", spectrum, in_factor, precision=highest)
    amplitude = lax.psum_scatter(partial_value, "col", scatter_dimension=1, tiled=True)
    amplitude = amplitude * kept_mask[None, None]
    column = first_col + jnp.arange(col_dev, dtype=jnp.int32)
    pick_y = (column[:, None] // modes_z == jnp.arange(modes_y, dtype=jnp.int32)[None, :]).astype(
        jnp.float32
    )
    pick_z = (column[:, None] % modes_z == jnp.arange(modes_z, dtype=jnp.int32)[None, :]).astype(
        jnp.float32
    )
    y_rows = jnp.dot(pick_y, y_factor, precision=highest)
    z_rows = jnp.dot(pick_z, z_factor, precision=highest)
    core_cols = jnp.einsum("prsabe,mb,me->prsam", tucker_core, y_rows, z_rows, precision=highest)
    kernel = jnp.einsum("prsam,ka->prskm", core_cols, x_factor, precision=highest)
    mixed_re = jnp.einsum("rskm,rkm->skm", kernel[0], amplitude[0], precision=highest) - jnp.einsum(
        "rskm,rkm->skm", kernel[1], amplitude[1], precision=highest
    )
    mixed_im = jnp.einsum("rskm,rkm->skm", kernel[0], amplitude[1], precision=highest) + jnp.einsum(
        "rskm,rkm->skm", kernel[1], amplitude[0], precision=highest
    )
    mixed_sum = lax.psum(jnp.stack([mixed_re, mixed_im]), "col")
    out_spec = jnp.einsum("os,qskm->qokm", out_factor, mixed_sum, precision=highest)
    x_backward = phase_table(jnp.arange(grid_x, dtype=jnp.int32), grid_x, modes_x, -1.0)
    x_values = jnp.einsum("pckm,xpqk->qcxm", out_spec, x_backward, precision=highest)
    returned = lax.all_to_all(x_values, "gx", split_axis=2, concat_axis=3, tiled=True)
    returned = returned.reshape(2, channels, planes, modes_y, modes_z)
    y_backward = phase_table(jnp.arange(grid_y, dtype=jnp.int32), grid_y, modes_y, -1.0)
    y_values = jnp.einsum("pcxjl,ypqj->cxqly", returned, y_backward, precision=highest)
    result = jnp.einsum("cxqly,qlz->cxyz", y_values, z_backward, precision=highest)
    return result.astype(jnp.bfloat16)


def solution(mesh):
    return jax.shard_map(
        per_device,
        mesh=mesh,
        in_specs=(
            P("col", "gx", None, None),
            P(None, "col", None, None, None, None),
            P("col", None),
            P("col", None),
            P(),
            P(),
            P(),
            P(),
        ),
        out_specs=P("col", "gx", None, None),
        check_vma=False,
    )
```

profile of v0, /device:TPU:0, one launch (start us, length us, event | category | flops | bytes accessed | tf_op | source)
XLA Modules:
  0.0 163.9 jit_solution(2289638814313260271)
XLA Ops:
  6.5 0.0 copy-start
  6.5 0.1 multiply_negate_fusion.1
  6.6 0.2 fusion.58
  6.8 6.5 %fusion = f32[2,16,16,4,256]{4,1,0,3,2:T(8,128)S(1)} fusion(bf16[16,4,256,128]{3,2,1,0:T(8,128)(2,1)} %param.8, f32[128,1,16]{0,2,1:T(8,128)S(1)} %get-tuple-element.35, f32[128,1,16]{0,2,1:T(8,128)S(1)} %get-tuple-element.36), kind=kOutput, calls=%fused_computation.3 | convolution fusion | flops 805310464 | bytes 6307840 | tf_op jit(solution)/shard_map/cxyz,zpl->cxply/dot_general | solution.py:53
  13.4 1.8 %fusion.9 = f32[2,16,4,32,16]{3,4,2,1,0:T(8,128)S(1)} fusion(f32[2,16,16,4,256]{4,1,0,3,2:T(8,128)S(1)} %fusion, f32[256,1,2,32]{0,3,1,2:T(8,128)S(1)} %get-tuple-element.14, f32[256,1,2,32]{0,3,1,2:T(8,128)S(1)} %get-tuple-element.15), kind=kOutput, calls=%fused_computation.19 | convolution fusion | flops 402685952 | bytes 2490368 | tf_op jit(solution)/shard_map/cxply,ypqj->qcxjl/dot_general | solution.py:54
  15.2 2.7 %copy.101 = f32[2,16,4,32,16]{1,2,0,4,3:T(4,128)} copy(f32[2,16,4,32,16]{3,4,2,1,0:T(8,128)S(1)} %fusion.9) | data formatting | bytes 524288 | tf_op jit(solution)/shard_map/reshape | solution.py:55
  17.9 0.0 copy-start.5
  17.9 3.8 %reshape.675 = f32[8,1,8192]{2,1,0:T(1,128)} reshape(f32[512,2,4,16]{3,2,1,0:T(4,128)} %bitcast.192) | data formatting | bytes 524288
  21.6 7.3 %all-to-all-start = ((f32[8,1,8192]{2,1,0:T(1,128)}), f32[8,1,8192]{2,1,0:T(1,128)S(1)}, u32[]{:S(2)}, u32[]{:S(2)}) async-start(f32[8,1,8192]{2,1,0:T(1,128)} %reshape.675), calls=%async_computation | async-start | bytes 524288 | tf_op jit(solution)/shard_map/all_to_all | solution.py:59
  28.9 0.0 reduce-scatter.2.cloned.1.call-start
  29.0 0.2 fusion.77
  29.2 0.0 copy-done.5
  29.2 0.2 fusion.40
  29.4 8.5 %all-to-all-done = f32[8,1,8192]{2,1,0:T(1,128)S(1)} async-done(((f32[8,1,8192]{2,1,0:T(1,128)}), f32[8,1,8192]{2,1,0:T(1,128)S(1)}, u32[]{:S(2)}, u32[]{:S(2)}) %all-to-all-start) | async-done | bytes 262176 | tf_op jit(solution)/shard_map/all_to_all | solution.py:59
  37.8 0.5 broadcast.967
  38.3 1.2 reduce.8
  39.5 2.8 %reshape.676 = f32[512,2,4,16]{3,2,1,0:T(4,128)} reshape(f32[8,8192]{1,0:T(8,128)S(1)} %reduce.8) | data formatting | bytes 524288
  42.3 0.0 copy-start.1
  42.3 1.9 %copy.103 = f32[2,16,4,8,64]{4,1,2,3,0:T(8,128)S(1)} copy(f32[2,16,4,8,64]{1,2,0,4,3:T(4,128)} %bitcast.191) | data formatting | bytes 524288 | tf_op jit(solution)/shard_map/all_to_all | solution.py:59
  44.2 0.0 copy-start.6
  44.2 0.0 copy-start.3
  44.2 0.7 convolution_bitcast_fusion.4
  44.9 0.0 copy-done.1
  44.9 2.2 %convolution_bitcast_fusion.2 = f32[2,32,32,64]{3,1,2,0:T(8,128)} fusion(f32[2,16,32,64]{3,2,1,0:T(8,128)S(1)} %convolution_bitcast_fusion.4, f32[16,32]{1,0:T(8,128)S(1)} %copy-done.1), kind=kOutput, calls=%fused_computation.18 | convolution fusion | flops 25165824 | bytes 788480 | tf_op jit(solution)/shard_map/qckm,cr->qrkm/dot_general | solution.py:61
  47.1 0.0 reduce-scatter.2.cloned.1.call-update
  47.2 0.2 all-reduce.2.cloned.1.call-start
  47.4 0.0 copy-done.6
  47.4 0.2 fusion.41
  47.6 0.0 copy-done.3
  47.6 0.1 copy.39
  47.7 0.1 reshape.644
  47.8 0.1 dynamic_slice.3
  47.9 0.0 copy-done
  47.9 0.0 copy-start.4
  47.9 3.7 %convolution_bitcast_fusion.1 = f32[2,8,32,8,64]{4,2,3,1,0:T(8,128)S(1)} fusion(f32[2,8,32,8,8,4]{2,5,4,3,1,0:T(4,128)S(1)} %copy-done, f32[64,8]{0,1:T(8,128)S(1)} %fusion.40, f32[64,4]{0,1:T(4,128)S(1)} %fusion.41), kind=kOutput, calls=%fused_computation.17 | convolution fusion | flops 100665344 | bytes 1575936 | tf_op jit(solution)/shard_map/prsabe,mb,me->prsam/dot_general | solution.py:73
  51.6 0.1 compare_convert_fusion
  51.7 0.0 copy-done.4
  51.7 9.0 %convolution_bitcast_fusion = f32[2,8,32,32,64]{4,3,2,1,0:T(8,128)} fusion(f32[2,8,32,8,64]{4,2,3,1,0:T(8,128)S(1)} %convolution_bitcast_fusion.1, f32[32,8]{0,1:T(8,128)S(1)} %copy-done.4), kind=kOutput, calls=%fused_computation.9 | convolution fusion | flops 100663296 | bytes 5243904 | tf_op jit(solution)/shard_map/prsam,ka->prskm/dot_general | solution.py:74
  60.7 10.5 %reduce-scatter.2.cloned.1.call-done = f32[2,8,32,64]{3,1,2,0:T(8,128)} async-done(((f32[2,32,32,64]{3,1,2,0:T(8,128)}), f32[2,8,32,64]{3,1,2,0:T(8,128)}) %reduce-scatter.2.cloned.1.call-update) | async-done | bytes 131088 | tf_op jit(solution)/shard_map/reduce_scatter | solution.py:62
  71.2 1.0 broadcast_multiply_fusion
  72.3 4.6 %multiply_reduce_fusion.3 = (f32[32,64,32]{1,0,2:T(8,128)S(1)}, f32[32,64,32]{1,0,2:T(8,128)S(1)}, f32[32,64,32]{1,0,2:T(8,128)S(1)}, f32[32,64,32]{1,0,2:T(8,128)S(1)}) fusion(f32[2,8,32,32,64]{4,3,2,1,0:T(8,128)} %convolution_bitcast_fusion, f32[32,64,8]{1,0,2:T(8,128)S(1)} %copy.107, f32[32,64,8]{1,0,2:T(8,128)S(1)} %copy.108), kind=kLoop, calls=%fused_computation.8 | loop fusion | flops 3932160 | bytes 5373952
  76.9 0.6 fusion.15
  77.5 0.0 copy-start.2
  77.5 0.6 fusion.14
  78.1 1.1 pad_maximum_fusion
  79.2 0.0 all-reduce.2.cloned.1.call-update
  79.2 36.5 %all-reduce.2.cloned.1.call-done = f32[2,32,32,64]{3,1,2,0:T(8,128)} async-done(((f32[2,32,32,64]{3,1,2,0:T(8,128)}), f32[2,32,32,64]{3,1,2,0:T(8,128)}) %all-reduce.2.cloned.1.call-update) | async-done | bytes 524304 | tf_op jit(solution)/shard_map/psum | solution.py:81
  115.7 0.0 copy-done.2
  115.7 1.9 %convolution_bitcast_fusion.5 = f32[2,16,32,64]{3,1,2,0:T(8,128)S(1)} fusion(f32[2,32,32,64]{3,1,2,0:T(8,128)} %all-reduce.2.cloned.1.call-done, f32[16,32]{1,0:T(8,128)S(1)} %copy-done.2), kind=kOutput, calls=%fused_computation.22 | convolution fusion | flops 25165824 | bytes 788480 | tf_op jit(solution)/shard_map/os,qskm->qokm/dot_general | solution.py:82
  117.6 0.7 convolution_bitcast_fusion.3
  118.3 0.3 copy.140
  118.6 1.0 reshape.677
  119.6 5.5 %all-to-all-start.1 = ((f32[8,1,8192]{2,1,0:T(1,128)}), f32[8,1,8192]{2,1,0:T(1,128)S(1)}, u32[]{:S(2)}, u32[]{:S(2)}) async-start(f32[8,1,8192]{2,1,0:T(1,128)} %reshape.677), calls=%async_computation.2 | async-start | bytes 524288 | tf_op jit(solution)/shard_map/all_to_all | solution.py:85
  125.2 0.1 cosine_multiply_fusion.2
  125.2 8.4 %all-to-all-done.1 = f32[8,1,8192]{2,1,0:T(1,128)S(1)} async-done(((f32[8,1,8192]{2,1,0:T(1,128)}), f32[8,1,8192]{2,1,0:T(1,128)S(1)}, u32[]{:S(2)}, u32[]{:S(2)}) %all-to-all-start.1) | async-done | bytes 262176 | tf_op jit(solution)/shard_map/all_to_all | solution.py:85
  133.6 1.2 reduce.9
  134.8 0.2 reshape.678
  135.0 0.3 copy.139
  135.3 1.8 %reshape.645 = f32[2,16,4,32,16]{4,3,2,1,0:T(8,128)} reshape(f32[2,16,4,8,64]{4,3,2,1,0:T(8,128)S(1)} %bitcast.194) | data formatting | bytes 524288 | tf_op jit(solution)/shard_map/reshape | solution.py:86
  137.1 5.1 %fusion.3 = f32[256,2,16,4,16,1]{0,4,1,5,3,2:T(8,128)S(1)} fusion(f32[256,1,2,32]{0,3,2,1:T(8,128)S(1)} %get-tuple-element.16, f32[256,1,2,32]{0,3,2,1:T(8,128)S(1)} %get-tuple-element.13, f32[2,16,4,32,16]{4,3,2,1,0:T(8,128)} %reshape.645), kind=kOutput, calls=%fused_computation.11 | convolution fusion | flops 402685952 | bytes 2490368 | tf_op jit(solution)/shard_map/pcxjl,ypqj->cxqly/dot_general | solution.py:88
  142.2 14.9 %bitcast_convert_fusion = bf16[16,4,256,128]{3,2,1,0:T(8,128)(2,1)} fusion(f32[256,2,16,4,16,1]{0,4,1,5,3,2:T(8,128)S(1)} %fusion.3, f32[1,16,128]{2,1,0:T(8,128)S(1)} %get-tuple-element.22, f32[1,16,128]{2,1,0:T(8,128)S(1)} %get-tuple-element.21), kind=kOutput, calls=%fused_computation | convolution fusion | flops 807407616 | bytes 6307840 | tf_op jit(solution)/shard_map/cxqly,qlz->cxyz/dot_general | solution.py:89
  (9 shorter events, 0.1 us)
Async XLA Ops:
  6.5 41.3 %copy-start = (f32[2,8,32,8,8,4]{2,5,4,3,1,0:T(4,128)S(1)}, f32[2,8,32,8,8,4]{2,5,4,3,1,0:T(4,128)}, u32[]{:S(2)}) copy-start(f32[2,8,32,8,8,4]{2,5,4,3,1,0:T(4,128)} %param.9) | copy-start | bytes 1572868
  17.9 11.3 %copy-start.5 = (f32[32,8]{0,1:T(8,128)S(1)}, f32[32,8]{0,1:T(8,128)}, u32[]{:S(2)}) copy-start(f32[32,8]{0,1:T(8,128)} %param.13) | copy-start | bytes 3076
  21.6 16.2 %all-to-all-start = ((f32[8,1,8192]{2,1,0:T(1,128)}), f32[8,1,8192]{2,1,0:T(1,128)S(1)}, u32[]{:S(2)}, u32[]{:S(2)}) async-start(f32[8,1,8192]{2,1,0:T(1,128)} %reshape.675), calls=%async_computation | async-start | bytes 524288 | tf_op jit(solution)/shard_map/all_to_all | solution.py:59
  28.9 42.3 %reduce-scatter.2.cloned.1.call-start = ((), (), s32[]{:S(2)}) async-start(), calls=%async_computation.3 | async-start | bytes 1310720 | tf_op jit(solution)/shard_map/reduce_scatter | solution.py:62
  42.3 2.6 %copy-start.1 = (f32[16,32]{1,0:T(8,128)S(1)}, f32[16,32]{1,0:T(8,128)}, u32[]{:S(2)}) copy-start(f32[16,32]{1,0:T(8,128)} %param.10) | copy-start | bytes 6148
  44.2 3.2 %copy-start.6 = (f32[16,4]{0,1:T(4,128)S(1)}, f32[16,4]{0,1:T(4,128)}, u32[]{:S(2)}) copy-start(f32[16,4]{0,1:T(4,128)} %param.14) | copy-start | bytes 772
  44.2 3.4 %copy-start.3 = (s32[32,16]{0,1:T(8,128)S(1)}, s32[32,16]{0,1:T(8,128)}, u32[]{:S(2)}) copy-start(s32[32,16]{0,1:T(8,128)} %param.15) | copy-start | bytes 6148
  47.2 68.5 %all-reduce.2.cloned.1.call-start = ((), (), s32[]{:S(2)}) async-start(), calls=%async_computation.4 | async-start | bytes 2097152 | tf_op jit(solution)/shard_map/psum | solution.py:81
  47.9 3.8 %copy-start.4 = (f32[32,8]{0,1:T(8,128)S(1)}, f32[32,8]{0,1:T(8,128)}, u32[]{:S(2)}) copy-start(f32[32,8]{0,1:T(8,128)} %param.12) | copy-start | bytes 3076
  77.5 38.2 %copy-start.2 = (f32[16,32]{1,0:T(8,128)S(1)}, f32[16,32]{1,0:T(8,128)}, u32[]{:S(2)}) copy-start(f32[16,32]{1,0:T(8,128)} %param.11) | copy-start | bytes 6148
  119.6 14.0 %all-to-all-start.1 = ((f32[8,1,8192]{2,1,0:T(1,128)}), f32[8,1,8192]{2,1,0:T(1,128)S(1)}, u32[]{:S(2)}, u32[]{:S(2)}) async-start(f32[8,1,8192]{2,1,0:T(1,128)} %reshape.677), calls=%async_computation.2 | async-start | bytes 524288 | tf_op jit(solution)/shard_map/all_to_all | solution.py:85
Sparse Core Ops, SparseCore 0:
  47.3 23.8 reduce-scatter.1
  79.3 36.2 all-reduce.1
where the time goes:
time: 164 us
  waiting for transfers between devices  63.9 us (39%)
  matrix products  46.9 us (29%)
  local copies, waits for them, and re-layouts  15.6 us (10%)
  between operations  13.6 us (8%)
  starting transfers between devices  13.1 us (8%)
  other arithmetic  10.8 us (7%)
    psum x1, waiting for transfers between devices, per_device(): mixed_sum = lax.psum(jnp.stack([mixed_re, mixed_im]), 'col')  36.5 us
    dot_general x1, matrix products, per_device(): jnp.einsum('cxqly,qlz->cxyz', y_values, z_backward, precision=highest)  14.9 us
    reduce_scatter x1, waiting for transfers between devices, per_device(): lax.psum_scatter(partial_value, 'col', scatter_dimension=1, tiled=True)  10.5 us
    dot_general x1, matrix products, per_device(): jnp.einsum('prsam,ka->prskm', core_cols, x_factor, precision=highest)  9.02 us
    all_to_all x1, waiting for transfers between devices, per_device(): lax.all_to_all(y_spectrum, 'gx', split_axis=3, concat_axis=2, tiled=True)  8.47 us
    all_to_all x1, waiting for transfers between devices, per_device(): lax.all_to_all(x_values, 'gx', split_axis=2, concat_axis=3, tiled=True)  8.4 us
    unnamed x22, local copies, waits for them, and re-layouts  7.99 us
    all_to_all x1, starting transfers between devices, per_device(): lax.all_to_all(y_spectrum, 'gx', split_axis=3, concat_axis=2, tiled=True)  7.29 us
  transfers between devices with their start and end apart: 4, of which 4 were waited for; matrix products, arithmetic and copies ran while one was open for 8% of the time, Pallas kernels for 0%

commit v1 on v0

--- a/solution.py
+++ b/solution.py
@@ -3,6 +3,7 @@
 import jax.numpy as jnp
 from jax import lax
 from jax.sharding import PartitionSpec as P
+from jax.lax import all_to_all, axis_size
 
 
 def slot_freq(slot_count):
@@ -82,7 +83,11 @@
     out_spec = jnp.einsum("os,qskm->qokm", out_factor, mixed_sum, precision=highest)
     x_backward = phase_table(jnp.arange(grid_x, dtype=jnp.int32), grid_x, modes_x, -1.0)
     x_values = jnp.einsum("pckm,xpqk->qcxm", out_spec, x_backward, precision=highest)
-    returned = lax.all_to_all(x_values, "gx", split_axis=2, concat_axis=3, tiled=True)
+    f_next = axis_size("gx")
+    v1 = jnp.split(x_values, f_next, axis=2)
+    known = jnp.stack(v1)
+    work_now = all_to_all(known, "gx", 0, 0)
+    returned = jnp.concatenate(work_now, 3)
     returned = returned.reshape(2, channels, planes, modes_y, modes_z)
     y_backward = phase_table(jnp.arange(grid_y, dtype=jnp.int32), grid_y, modes_y, -1.0)
     y_values = jnp.einsum("pcxjl,ypqj->cxqly", returned, y_backward, precision=highest)

time: 164 us -> 165 us (level)
    another operation x0 -> x2, local copies, waits for them, and re-layouts: none -> 1.82 us  [the longest x1 1.79 us: per_device(): returned = returned.reshape(2, channels, planes, modes_y, modes_z)]
    unnamed x22 -> x29, local copies, waits for them, and re-layouts: 7.99 us -> 8.5 us
where the time goes in v1:
time: 165 us; the launch traced here: 164 us
  waiting for transfers between devices  63.9 us (39%)
  matrix products  46.9 us (28%)
  local copies, waits for them, and re-layouts  15.8 us (10%)
  between operations  13.6 us (8%)
  starting transfers between devices  13.1 us (8%)
  other arithmetic  10.8 us (7%)
    psum x1, waiting for transfers between devices, per_device(): mixed_sum = lax.psum(jnp.stack([mixed_re, mixed_im]), 'col')  36.5 us
    dot_general x1, matrix products, per_device(): jnp.einsum('cxqly,qlz->cxyz', y_values, z_backward, precision=highest)  14.9 us
    reduce_scatter x1, waiting for transfers between devices, per_device(): lax.psum_scatter(partial_value, 'col', scatter_dimension=1, tiled=True)  10.5 us
    dot_general x1, matrix products, per_device(): jnp.einsum('prsam,ka->prskm', core_cols, x_factor, precision=highest)  9.02 us
    unnamed x29, local copies, waits for them, and re-layouts  8.5 us
    all_to_all x1, waiting for transfers between devices, per_device(): lax.all_to_all(y_spectrum, 'gx', split_axis=3, concat_axis=2, tiled=True)  8.47 us
    all_to_all x1, waiting for transfers between devices, per_device(): work_now = all_to_all(known, 'gx', 0, 0)  8.4 us
    all_to_all x1, starting transfers between devices, per_device(): lax.all_to_all(y_spectrum, 'gx', split_axis=3, concat_axis=2, tiled=True)  7.29 us
  transfers between devices with their start and end apart: 4, of which 4 were waited for; matrix products, arithmetic and copies ran while one was open for 8% of the time, Pallas kernels for 0%

profile of v1, /device:TPU:0, one launch (start us, length us, event | category | flops | bytes accessed | tf_op | source)
XLA Modules:
  0.0 164.1 jit_solution(13735980997955982344)
XLA Ops:
  6.5 0.0 copy-start
  6.5 0.1 multiply_negate_fusion.1
  6.6 0.2 fusion.66
  6.8 6.5 %fusion = f32[2,16,16,4,256]{4,1,0,3,2:T(8,128)S(1)} fusion(bf16[16,4,256,128]{3,2,1,0:T(8,128)(2,1)} %param.8, f32[128,1,16]{0,2,1:T(8,128)S(1)} %get-tuple-element.35, f32[128,1,16]{0,2,1:T(8,128)S(1)} %get-tuple-element.36), kind=kOutput, calls=%fused_computation.3 | convolution fusion | flops 805310464 | bytes 6307840 | tf_op jit(solution)/shard_map/cxyz,zpl->cxply/dot_general | solution.py:54
  13.4 1.8 %fusion.9 = f32[2,16,4,32,16]{3,4,2,1,0:T(8,128)S(1)} fusion(f32[2,16,16,4,256]{4,1,0,3,2:T(8,128)S(1)} %fusion, f32[256,1,2,32]{0,3,1,2:T(8,128)S(1)} %get-tuple-element.14, f32[256,1,2,32]{0,3,1,2:T(8,128)S(1)} %get-tuple-element.15), kind=kOutput, calls=%fused_computation.19 | convolution fusion | flops 402685952 | bytes 2490368 | tf_op jit(solution)/shard_map/cxply,ypqj->qcxjl/dot_general | solution.py:55
  15.2 2.7 %copy.99 = f32[2,16,4,32,16]{1,2,0,4,3:T(4,128)} copy(f32[2,16,4,32,16]{3,4,2,1,0:T(8,128)S(1)} %fusion.9) | data formatting | bytes 524288 | tf_op jit(solution)/shard_map/reshape | solution.py:56
  17.9 0.0 copy-start.5
  17.9 3.8 %reshape.674 = f32[8,1,8192]{2,1,0:T(1,128)} reshape(f32[512,2,4,16]{3,2,1,0:T(4,128)} %bitcast.217) | data formatting | bytes 524288
  21.6 7.3 %all-to-all-start = ((f32[8,1,8192]{2,1,0:T(1,128)}), f32[8,1,8192]{2,1,0:T(1,128)S(1)}, u32[]{:S(2)}, u32[]{:S(2)}) async-start(f32[8,1,8192]{2,1,0:T(1,128)} %reshape.674), calls=%async_computation | async-start | bytes 524288 | tf_op jit(solution)/shard_map/all_to_all | solution.py:60
  28.9 0.0 reduce-scatter.2.cloned.1.call-start
  29.0 0.2 fusion.85
  29.2 0.0 copy-done.5
  29.2 0.2 fusion.48
  29.4 8.5 %all-to-all-done = f32[8,1,8192]{2,1,0:T(1,128)S(1)} async-done(((f32[8,1,8192]{2,1,0:T(1,128)}), f32[8,1,8192]{2,1,0:T(1,128)S(1)}, u32[]{:S(2)}, u32[]{:S(2)}) %all-to-all-start) | async-done | bytes 262176 | tf_op jit(solution)/shard_map/all_to_all | solution.py:60
  37.8 0.5 broadcast.967
  38.3 1.2 reduce.8
  39.5 2.8 %reshape.675 = f32[512,2,4,16]{3,2,1,0:T(4,128)} reshape(f32[8,8192]{1,0:T(8,128)S(1)} %reduce.8) | data formatting | bytes 524288
  42.3 0.0 copy-start.1
  42.3 1.9 %copy.101 = f32[2,16,4,8,64]{4,1,2,3,0:T(8,128)S(1)} copy(f32[2,16,4,8,64]{1,2,0,4,3:T(4,128)} %bitcast.216) | data formatting | bytes 524288 | tf_op jit(solution)/shard_map/all_to_all | solution.py:60
  44.2 0.0 copy-start.6
  44.2 0.0 copy-start.3
  44.2 0.7 convolution_bitcast_fusion.4
  44.9 0.0 copy-done.1
  44.9 2.2 %convolution_bitcast_fusion.2 = f32[2,32,32,64]{3,1,2,0:T(8,128)} fusion(f32[2,16,32,64]{3,2,1,0:T(8,128)S(1)} %convolution_bitcast_fusion.4, f32[16,32]{1,0:T(8,128)S(1)} %copy-done.1), kind=kOutput, calls=%fused_computation.18 | convolution fusion | flops 25165824 | bytes 788480 | tf_op jit(solution)/shard_map/qckm,cr->qrkm/dot_general | solution.py:62
  47.1 0.0 reduce-scatter.2.cloned.1.call-update
  47.2 0.2 all-reduce.2.cloned.1.call-start
  47.4 0.0 copy-done.6
  47.4 0.2 fusion.49
  47.6 0.0 copy-done.3
  47.6 0.1 copy.38
  47.7 0.1 reshape.643
  47.8 0.1 dynamic_slice.3
  47.9 0.0 copy-done
  47.9 0.0 copy-start.4
  47.9 3.7 %convolution_bitcast_fusion.1 = f32[2,8,32,8,64]{4,2,3,1,0:T(8,128)S(1)} fusion(f32[2,8,32,8,8,4]{2,5,4,3,1,0:T(4,128)S(1)} %copy-done, f32[64,8]{0,1:T(8,128)S(1)} %fusion.48, f32[64,4]{0,1:T(4,128)S(1)} %fusion.49), kind=kOutput, calls=%fused_computation.17 | convolution fusion | flops 100665344 | bytes 1575936 | tf_op jit(solution)/shard_map/prsabe,mb,me->prsam/dot_general | solution.py:74
  51.6 0.1 compare_convert_fusion
  51.7 0.0 copy-done.4
  51.7 9.0 %convolution_bitcast_fusion = f32[2,8,32,32,64]{4,3,2,1,0:T(8,128)} fusion(f32[2,8,32,8,64]{4,2,3,1,0:T(8,128)S(1)} %convolution_bitcast_fusion.1, f32[32,8]{0,1:T(8,128)S(1)} %copy-done.4), kind=kOutput, calls=%fused_computation.9 | convolution fusion | flops 100663296 | bytes 5243904 | tf_op jit(solution)/shard_map/prsam,ka->prskm/dot_general | solution.py:75
  60.7 10.5 %reduce-scatter.2.cloned.1.call-done = f32[2,8,32,64]{3,1,2,0:T(8,128)} async-done(((f32[2,32,32,64]{3,1,2,0:T(8,128)}), f32[2,8,32,64]{3,1,2,0:T(8,128)}) %reduce-scatter.2.cloned.1.call-update) | async-done | bytes 131088 | tf_op jit(solution)/shard_map/reduce_scatter | solution.py:63
  71.2 1.0 broadcast_multiply_fusion
  72.3 4.6 %multiply_reduce_fusion.3 = (f32[32,64,32]{1,0,2:T(8,128)S(1)}, f32[32,64,32]{1,0,2:T(8,128)S(1)}, f32[32,64,32]{1,0,2:T(8,128)S(1)}, f32[32,64,32]{1,0,2:T(8,128)S(1)}) fusion(f32[2,8,32,32,64]{4,3,2,1,0:T(8,128)} %convolution_bitcast_fusion, f32[32,64,8]{1,0,2:T(8,128)S(1)} %copy.105, f32[32,64,8]{1,0,2:T(8,128)S(1)} %copy.106), kind=kLoop, calls=%fused_computation.8 | loop fusion | flops 3932160 | bytes 5373952
  76.9 0.6 fusion.15
  77.5 0.0 copy-start.2
  77.5 0.6 fusion.14
  78.1 1.1 pad_maximum_fusion
  79.2 0.0 all-reduce.2.cloned.1.call-update
  79.2 36.5 %all-reduce.2.cloned.1.call-done = f32[2,32,32,64]{3,1,2,0:T(8,128)} async-done(((f32[2,32,32,64]{3,1,2,0:T(8,128)}), f32[2,32,32,64]{3,1,2,0:T(8,128)}) %all-reduce.2.cloned.1.call-update) | async-done | bytes 524304 | tf_op jit(solution)/shard_map/psum | solution.py:82
  115.7 0.0 copy-done.2
  115.7 1.9 %convolution_bitcast_fusion.5 = f32[2,16,32,64]{3,1,2,0:T(8,128)S(1)} fusion(f32[2,32,32,64]{3,1,2,0:T(8,128)} %all-reduce.2.cloned.1.call-done, f32[16,32]{1,0:T(8,128)S(1)} %copy-done.2), kind=kOutput, calls=%fused_computation.22 | convolution fusion | flops 25165824 | bytes 788480 | tf_op jit(solution)/shard_map/os,qskm->qokm/dot_general | solution.py:83
  117.6 0.7 convolution_bitcast_fusion.3
  118.5 1.2 reshape.676
  119.7 5.5 %all-to-all-start.1 = ((f32[8,1,8192]{2,1,0:T(1,128)}), f32[8,1,8192]{2,1,0:T(1,128)S(1)}, u32[]{:S(2)}, u32[]{:S(2)}) async-start(f32[8,1,8192]{2,1,0:T(1,128)} %reshape.676), calls=%async_computation.2 | async-start | bytes 524288 | tf_op jit(solution)/shard_map/all_to_all | solution.py:89
  125.3 0.1 cosine_multiply_fusion.2
  125.3 8.4 %all-to-all-done.1 = f32[8,1,8192]{2,1,0:T(1,128)S(1)} async-done(((f32[8,1,8192]{2,1,0:T(1,128)}), f32[8,1,8192]{2,1,0:T(1,128)S(1)}, u32[]{:S(2)}, u32[]{:S(2)}) %all-to-all-start.1) | async-done | bytes 262176 | tf_op jit(solution)/shard_map/all_to_all | solution.py:89
  133.7 1.2 reduce.9
  134.9 0.3 reshape.677
  135.3 0.3 copy.42
  135.6 1.8 %reshape_reshape.3 = f32[2,16,4,32,16]{4,3,2,1,0:T(8,128)} reshape(f32[2,16,4,8,64]{4,3,2,1,0:T(8,128)S(1)} %copy.42) | data formatting | bytes 524288 | tf_op jit(solution)/shard_map/reshape;reshape | solution.py:91
  137.4 5.1 %fusion.3 = f32[256,2,16,4,16,1]{0,4,1,5,3,2:T(8,128)S(1)} fusion(f32[256,1,2,32]{0,3,2,1:T(8,128)S(1)} %get-tuple-element.16, f32[256,1,2,32]{0,3,2,1:T(8,128)S(1)} %get-tuple-element.13, f32[2,16,4,32,16]{4,3,2,1,0:T(8,128)} %reshape_reshape.3), kind=kOutput, calls=%fused_computation.11 | convolution fusion | flops 402685952 | bytes 2490368 | tf_op jit(solution)/shard_map/pcxjl,ypqj->cxqly/dot_general | solution.py:93
  142.4 14.9 %bitcast_convert_fusion = bf16[16,4,256,128]{3,2,1,0:T(8,128)(2,1)} fusion(f32[256,2,16,4,16,1]{0,4,1,5,3,2:T(8,128)S(1)} %fusion.3, f32[1,16,128]{2,1,0:T(8,128)S(1)} %get-tuple-element.22, f32[1,16,128]{2,1,0:T(8,128)S(1)} %get-tuple-element.21), kind=kOutput, calls=%fused_computation | convolution fusion | flops 807407616 | bytes 6307840 | tf_op jit(solution)/shard_map/cxqly,qlz->cxyz/dot_general | solution.py:94
  (17 shorter events, 0.4 us)
Async XLA Ops:
  6.5 41.3 %copy-start = (f32[2,8,32,8,8,4]{2,5,4,3,1,0:T(4,128)S(1)}, f32[2,8,32,8,8,4]{2,5,4,3,1,0:T(4,128)}, u32[]{:S(2)}) copy-start(f32[2,8,32,8,8,4]{2,5,4,3,1,0:T(4,128)} %param.9) | copy-start | bytes 1572868
  17.9 11.3 %copy-start.5 = (f32[32,8]{0,1:T(8,128)S(1)}, f32[32,8]{0,1:T(8,128)}, u32[]{:S(2)}) copy-start(f32[32,8]{0,1:T(8,128)} %param.13) | copy-start | bytes 3076
  21.6 16.2 %all-to-all-start = ((f32[8,1,8192]{2,1,0:T(1,128)}), f32[8,1,8192]{2,1,0:T(1,128)S(1)}, u32[]{:S(2)}, u32[]{:S(2)}) async-start(f32[8,1,8192]{2,1,0:T(1,128)} %reshape.674), calls=%async_computation | async-start | bytes 524288 | tf_op jit(solution)/shard_map/all_to_all | solution.py:60
  28.9 42.3 %reduce-scatter.2.cloned.1.call-start = ((), (), s32[]{:S(2)}) async-start(), calls=%async_computation.3 | async-start | bytes 1310720 | tf_op jit(solution)/shard_map/reduce_scatter | solution.py:63
  42.3 2.6 %copy-start.1 = (f32[16,32]{1,0:T(8,128)S(1)}, f32[16,32]{1,0:T(8,128)}, u32[]{:S(2)}) copy-start(f32[16,32]{1,0:T(8,128)} %param.10) | copy-start | bytes 6148
  44.2 3.2 %copy-start.6 = (f32[16,4]{0,1:T(4,128)S(1)}, f32[16,4]{0,1:T(4,128)}, u32[]{:S(2)}) copy-start(f32[16,4]{0,1:T(4,128)} %param.14) | copy-start | bytes 772
  44.2 3.4 %copy-start.3 = (s32[32,16]{0,1:T(8,128)S(1)}, s32[32,16]{0,1:T(8,128)}, u32[]{:S(2)}) copy-start(s32[32,16]{0,1:T(8,128)} %param.15) | copy-start | bytes 6148
  47.2 68.5 %all-reduce.2.cloned.1.call-start = ((), (), s32[]{:S(2)}) async-start(), calls=%async_computation.4 | async-start | bytes 2097152 | tf_op jit(solution)/shard_map/psum | solution.py:82
  47.9 3.8 %copy-start.4 = (f32[32,8]{0,1:T(8,128)S(1)}, f32[32,8]{0,1:T(8,128)}, u32[]{:S(2)}) copy-start(f32[32,8]{0,1:T(8,128)} %param.12) | copy-start | bytes 3076
  77.5 38.2 %copy-start.2 = (f32[16,32]{1,0:T(8,128)S(1)}, f32[16,32]{1,0:T(8,128)}, u32[]{:S(2)}) copy-start(f32[16,32]{1,0:T(8,128)} %param.11) | copy-start | bytes 6148
  119.7 14.0 %all-to-all-start.1 = ((f32[8,1,8192]{2,1,0:T(1,128)}), f32[8,1,8192]{2,1,0:T(1,128)S(1)}, u32[]{:S(2)}, u32[]{:S(2)}) async-start(f32[8,1,8192]{2,1,0:T(1,128)} %reshape.676), calls=%async_computation.2 | async-start | bytes 524288 | tf_op jit(solution)/shard_map/all_to_all | solution.py:89
Sparse Core Ops, SparseCore 0:
  47.3 23.8 reduce-scatter.1
  79.3 36.2 all-reduce.1
